TPU v7x, 16 devices: a 4x2x1 block of a 4x4x8 slice. The times are simulated.
16 devices in a mesh: dp: 2 (over y, z), tp: 8 (over x, core).
Axes of the slice: x: 4, y: 2, z: 1, core: 2. Of those that a mesh axis runs over, the one named last changes fastest.
The devices are a block of a 4x4x8 slice.
Arguments:
- x_seq: bfloat16 [4, 2048, 4096], P('dp', 'tp'), parts along dimension 0
- ln_gain: bfloat16 [4096], replicated
- w_qkv: bfloat16 [4096, 8, 768], P(None, 'tp')
- w_out: bfloat16 [4096, 4096], P('tp')
- y_grad: bfloat16 [4, 2048, 4096], P('dp', 'tp'), parts along dimension 0
Outputs:
- output 1: bfloat16 [4, 2048, 4096], P('dp', 'tp'), parts along dimension 0
- output 2: bfloat16 [4, 2048, 4096], P('dp', 'tp'), parts along dimension 0
- output 3: bfloat16 [8192], P('dp'), parts along dimension 0
- output 4: bfloat16 [8192, 8, 768], P('dp', 'tp'), parts along dimension 0
- output 5: bfloat16 [8192, 4096], P(('dp', 'tp')), parts along dimension 0
There are 2 independent parts. A program takes and returns all parts, laid end to end along the dimension named above; an argument that names none is the same for every part.
All inputs are finite; a program needn't handle non-finite values.
Results may differ from a plain program's by a relative error of at most 0.0177313.
Values are sent between devices in bfloat16 or wider.
A program may use at most 768 MiB of HBM per device.

v0:
```python
import functools
import jax
import jax.numpy as jnp
from jax import lax
from jax.sharding import PartitionSpec as P

CLIP_QKV = 8.0
ROPE_THETA = 500000.0
LN_EPS = 1e-5


def layer_norm(x_f32, gain_f32):
    row_mean = jnp.mean(x_f32, axis=-1, keepdims=True)
    centered = x_f32 - row_mean
    variance = jnp.mean(centered * centered, axis=-1, keepdims=True)
    return (centered * lax.rsqrt(variance + LN_EPS) * gain_f32).astype(jnp.bfloat16)


def rope_tables(positions, head_dim):
    inv_freq = 1.0 / (ROPE_THETA ** (jnp.arange(0, head_dim, 2, dtype=jnp.float32) / head_dim))
    angles = positions.astype(jnp.float32)[:, None] * inv_freq[None, :]
    return jnp.cos(angles), jnp.sin(angles)


def rotate(vec_in, cos_t, sin_t):
    half_dim = vec_in.shape[-1] // 2
    half_lo = vec_in[..., :half_dim]
    half_hi = vec_in[..., half_dim:]
    return jnp.concatenate([half_lo * cos_t - half_hi * sin_t, half_hi * cos_t + half_lo * sin_t], axis=-1)


def attention_core(qkv_clip, head_dim):
    batch_n, seq_len, kv_loc, slot_width = qkv_clip.shape
    groups = slot_width // head_dim - 2
    qkv_slots = qkv_clip.reshape(batch_n, seq_len, kv_loc, groups + 2, head_dim)
    cos_t, sin_t = rope_tables(jnp.arange(seq_len), head_dim)
    query_rot = rotate(qkv_slots[:, :, :, :groups].astype(jnp.float32), cos_t[:, None, None], sin_t[:, None, None]).astype(jnp.bfloat16)
    key_rot = rotate(qkv_slots[:, :, :, groups].astype(jnp.float32), cos_t[:, None], sin_t[:, None]).astype(jnp.bfloat16)
    val_head = qkv_slots[:, :, :, groups + 1]
    scores = jnp.einsum('bqngd,bknd->bngqk', query_rot, key_rot, preferred_element_type=jnp.float32) * head_dim ** -0.5
    causal = jnp.arange(seq_len)[:, None] >= jnp.arange(seq_len)[None, :]
    scores = jnp.where(causal, scores, -1e30)
    attn_prob = jax.nn.softmax(scores, axis=-1).astype(jnp.bfloat16)
    mixed = jnp.einsum('bngqk,bknd->bqngd', attn_prob, val_head, preferred_element_type=jnp.float32).astype(jnp.bfloat16)
    return mixed.reshape(batch_n, seq_len, kv_loc * groups * head_dim)


def solution(mesh):
    def device_step(x_seq, ln_gain, w_qkv, w_out, y_grad):
        kv_loc = w_qkv.shape[1]
        head_dim = (w_qkv.shape[2] - w_out.shape[0] // kv_loc) // 2
        x_f32 = x_seq.astype(jnp.float32)
        h_loc, norm_pullback = jax.vjp(layer_norm, x_f32, ln_gain.astype(jnp.float32))
        h_full = lax.all_gather(h_loc, 'tp', axis=1, tiled=True)
        qkv_raw = jnp.einsum('bsd,dnc->bsnc', h_full, w_qkv, preferred_element_type=jnp.float32).astype(jnp.bfloat16)
        qkv_clip = jnp.minimum(jnp.maximum(qkv_raw, -CLIP_QKV), CLIP_QKV)
        attn_out, core_pullback = jax.vjp(functools.partial(attention_core, head_dim=head_dim), qkv_clip)
        out_part = jnp.einsum('bsk,kd->bsd', attn_out, w_out, preferred_element_type=jnp.float32).astype(jnp.bfloat16)
        out_loc = lax.psum_scatter(out_part, 'tp', scatter_dimension=1, tiled=True)
        y_out = (x_f32 + out_loc.astype(jnp.float32)).astype(jnp.bfloat16)
        grad_full = lax.all_gather(y_grad, 'tp', axis=1, tiled=True)
        wout_grad = jnp.einsum('bsk,bsd->kd', attn_out, grad_full, preferred_element_type=jnp.float32).astype(jnp.bfloat16)
        d_attn = jnp.einsum('bsd,kd->bsk', grad_full, w_out, preferred_element_type=jnp.float32).astype(jnp.bfloat16)
        (d_clip,) = core_pullback(d_attn)
        d_qkv = jnp.where(jnp.abs(qkv_raw) < CLIP_QKV, d_clip, jnp.zeros_like(d_clip))
        wqkv_grad = jnp.einsum('bsd,bsnc->dnc', h_full, d_qkv, preferred_element_type=jnp.float32).astype(jnp.bfloat16)
        dh_part = jnp.einsum('bsnc,dnc->bsd', d_qkv, w_qkv, preferred_element_type=jnp.float32).astype(jnp.bfloat16)
        dh_loc = lax.psum_scatter(dh_part, 'tp', scatter_dimension=1, tiled=True)
        dx_norm, gain_part = norm_pullback(dh_loc)
        x_grad = (y_grad.astype(jnp.float32) + dx_norm).astype(jnp.bfloat16)
        gain_grad = lax.psum(gain_part, 'tp').astype(jnp.bfloat16)
        return y_out, x_grad, gain_grad, wqkv_grad, wout_grad

    specs_in = (P('dp', 'tp', None), P(None), P(None, 'tp', None), P('tp', None), P('dp', 'tp', None))
    specs_out = (P('dp', 'tp', None), P('dp', 'tp', None), P('dp'), P('dp', 'tp', None), P(('dp', 'tp'), None))
    return jax.shard_map(device_step, mesh=mesh, in_specs=specs_in, out_specs=specs_out, check_vma=False)
```

profile of v0, /device:TPU:112, one launch (start us, length us, event | category | flops | bytes accessed | tf_op | source)
XLA Modules:
  0.0 1068.7 jit_solution(9915052834384364474)
XLA Ops:
  7.2 0.0 copy-start.25
  7.2 0.1 all-gather.3.cloned.1.call-start
  7.3 0.0 copy-start
  7.3 3.0 convert_reduce_fusion
  10.3 3.4 fusion.27
  13.7 0.6 copy-done.23
  14.3 0.0 copy-done.25
  14.3 0.6 copy-done.21
  14.8 0.6 copy-done.14
  15.4 4.4 fusion.25
  19.8 0.1 all-gather.3.cloned.1.call-update
  19.9 0.1 all-gather.5.cloned.1.call-start
  20.0 0.7 all-gather.5.cloned.1.call-update
  20.7 0.1 reduce-scatter.5.cloned.1.call-start
  20.8 3.7 multiply_cosine_fusion
  24.5 4.1 iota_compare_fusion
  28.6 146.9 %all-gather.3.cloned.1.call-done = bf16[2,2048,4096]{2,1,0:T(8,128)(2,1)} async-done(((bf16[2,256,4096]{2,1,0:T(8,128)(2,1)}), bf16[2,2048,4096]{2,1,0:T(8,128)(2,1)}) %all-gather.3.cloned.1.call-update) | async-done | bytes 33554448 | tf_op jit(solution)/shard_map/all_gather | solution.py:54
  175.6 34.2 %broadcast_clamp_fusion = (bf16[2,2048,768]{1,2,0:T(8,128)(2,1)}, bf16[2,2048,768]{1,2,0:T(8,128)(2,1)}) fusion(bf16[2,2048,4096]{2,1,0:T(8,128)(2,1)} %all-gather.3.cloned.1.call-done, bf16[4096,1,768]{2,0,1:T(8,128)(2,1)} %param.7), kind=kOutput, calls=%fused_computation.72 | convolution fusion | flops 25776095232 | bytes 52428800 | tf_op jit(solution)/shard_map/bsd,dnc->bsnc/dot_general | solution.py:55
  209.8 2.3 slice.29
  212.1 4.8 slice.32
  216.9 1.6 copy.50
  218.5 6.2 copy.51
  224.7 2.7 convert_element_type.176
  227.4 0.1 bitcast_convert_fusion.3
  227.6 1.8 fusion.80
  229.3 0.0 copy-done.3
  229.4 5.0 fusion.38
  234.3 0.0 copy-done.11
  234.3 54.5 %fusion.9 = (f32[2,4,2048]{2,1,0:T(4,128)S(1)}, f32[2,2048,2048,4]{2,1,3,0:T(8,128)}) fusion(pred[2048,2048]{0,1:T(8,128)(4,1)} %iota_compare_fusion, bf16[2,2048,4,64]{3,1,2,0:T(8,128)(2,1)} %get-tuple-element.10, bf16[2,2048,4,64]{3,1,2,0:T(8,128)(2,1)} %get-tuple-element.9, bf16[2,2048,64]{2,1,0:T(8,128)(2,1)} %get-tuple-element.16, ...), kind=kOutput, calls=%fused_computation.14 | convolution fusion | flops 8701067264 | bytes 143720448 | tf_op jit(solution)/shard_map/jvp(bqngd,bknd->bngqk)/dot_general | solution.py:40
  288.8 42.4 %fusion.56 = f32[2,4,2048]{2,1,0:T(4,128)S(1)} fusion(f32[2,4,2048]{2,1,0:T(4,128)S(1)} %get-tuple-element.21, f32[2,2048,2048,4]{2,1,3,0:T(8,128)} %get-tuple-element.22, pred[2048,2048]{0,1:T(8,128)(4,1)} %iota_compare_fusion), kind=kLoop, calls=%fused_computation.73 | loop fusion | flops 134201344 | bytes 138543104 | tf_op jit(solution)/shard_map/jvp()/reduce_sum | solution.py:43
  331.2 0.6 multiply_divide_fusion
  331.9 23.8 %fusion.48 = bf16[2,2048,512]{1,2,0:T(8,128)(2,1)} fusion(bf16[2,2048,4096]{2,1,0:T(8,128)(2,1)} %all-gather.5.cloned.1.call-done, bf16[512,4096]{1,0:T(8,128)(2,1)} %param.8), kind=kOutput, calls=%fused_computation.68 | convolution fusion | flops 17181966336 | bytes 41943040 | tf_op jit(solution)/shard_map/bsd,kd->bsk/dot_general | solution.py:63
  355.6 48.4 %fusion.75 = bf16[2,2048,1,1,128]{4,1,3,0,2:T(8,128)(2,1)} fusion(bf16[2,128,4,2048]{3,1,2,0:T(8,128)(2,1)} %bitcast.246, f32[2,4,2048]{2,1,0:T(4,128)S(1)} %fusion.56, f32[2,4,2048]{2,1,0:T(4,128)S(1)} %get-tuple-element.21, f32[2,2048,2048,4]{2,1,3,0:T(8,128)} %get-tuple-element.22, pred[2048,2048]{0,1:T(8,128)(4,1)} %iota_compare_fusion), kind=kOutput, calls=%fused_computation.80 | convolution fusion | flops 8758231040 | bytes 143785984 | tf_op jit(solution)/shard_map/transpose(jvp(bngqk,bknd->bqngd))/dot_general | solution.py:44
  404.1 0.0 copy-done.20
  404.1 78.2 %fusion.8 = (f32[2,4,2048]{2,1,0:T(4,128)S(1)}, bf16[2,4,2048,2048]{2,3,1,0:T(8,128)(2,1)}) fusion(f32[2,4,2048]{2,1,0:T(4,128)S(1)} %copy-done.20, f32[2,4,2048]{2,1,0:T(4,128)S(1)} %get-tuple-element.21, f32[2,2048,2048,4]{2,1,3,0:T(8,128)} %get-tuple-element.22, pred[2048,2048]{0,1:T(8,128)(4,1)} %iota_compare_fusion, ...), kind=kOutput, calls=%fused_computation.10 | convolution fusion | flops 8858353664 | bytes 210960384 | tf_op jit(solution)/shard_map/transpose(jvp(bngqk,bknd->bqngd))/dot_general | solution.py:44
  482.3 83.0 %fusion.72 = f32[2,2048,1,128]{3,1,0,2:T(8,128)} fusion(bf16[2,4,2048,2048]{2,3,1,0:T(8,128)(2,1)} %get-tuple-element.24, f32[2,4,2048]{2,1,0:T(4,128)S(1)} %neg.16, f32[2,4,2048]{2,1,0:T(4,128)S(1)} %copy-done.17, pred[2048,2048]{0,1:T(8,128)(4,1)} %iota_compare_fusion, f32[2,4,2048]{2,1,0:T(4,128)S(1)} %get-tuple-element.21, ...), kind=kOutput, calls=%fused_computation.79 | convolution fusion | flops 8901361664 | bytes 212008960 | tf_op jit(solution)/shard_map/transpose(jvp(bqngd,bknd->bngqk))/dot_general | solution.py:40
  565.4 79.9 %bitcast_convert_fusion.2 = f32[2,2048,1,4,128]{4,1,3,0,2:T(8,128)} fusion(bf16[2,4,2048,2048]{2,3,1,0:T(8,128)(2,1)} %get-tuple-element.24, f32[2,4,2048]{2,1,0:T(4,128)S(1)} %neg.16, f32[2,4,2048]{2,1,0:T(4,128)S(1)} %copy-done.17, pred[2048,2048]{0,1:T(8,128)(4,1)} %iota_compare_fusion, f32[2,2048,2048,4]{2,1,3,0:T(8,128)} %get-tuple-element.22, ...), kind=kOutput, calls=%fused_computation.63 | convolution fusion | flops 8898215936 | bytes 215154688 | tf_op jit(solution)/shard_map/transpose(jvp(bqngd,bknd->bngqk))/dot_general | solution.py:40
  645.3 7.6 fusion.53
  652.9 0.0 copy-done.6
  652.9 2.6 multiply_add_fusion.3
  655.6 7.2 multiply_add_fusion.1
  662.7 2.8 fusion.82
  665.6 0.0 copy-start.10
  665.6 2.3 add_convert_fusion.1
  667.9 0.0 copy-done.10
  668.0 3.0 pad_add_fusion
  671.0 8.9 copy.23
  679.9 34.6 %convolution_convert_fusion.2 = bf16[2,2048,4096]{2,1,0:T(8,128)(2,1)} fusion(bf16[4096,1,768]{2,0,1:T(8,128)(2,1)} %param.7, bf16[2,2048,768]{1,2,0:T(8,128)(2,1)} %bitcast.238, u8[2048,768]{0,1:T(8,128)(4,1)S(1)} %copy-done.8), kind=kOutput, calls=%fused_computation.23 | convolution fusion | flops 25802309632 | bytes 47710208 | tf_op jit(solution)/shard_map/bsnc,dnc->bsd/dot_general | solution.py:67
  714.5 0.1 reduce-scatter.5.cloned.1.call-update
  714.6 0.1 reduce-scatter.3.cloned.1.call-start
  714.7 0.0 copy-start.26
  714.7 50.3 %fusion.45 = bf16[2,128,4,2048]{3,1,2,0:T(8,128)(2,1)} fusion(bf16[2,2048,1,6,128]{1,4,3,0,2:T(8,128)(2,1)} %bitcast.243, f32[2,4,2048]{2,1,0:T(4,128)S(1)} %copy-done.17, f32[2,4,2048]{2,1,0:T(4,128)S(1)} %get-tuple-element.21, f32[2,2048,2048,4]{2,1,3,0:T(8,128)} %get-tuple-element.22, pred[2048,2048]{0,1:T(8,128)(4,1)} %iota_compare_fusion), kind=kOutput, calls=%fused_computation.67 | convolution fusion | flops 8759803904 | bytes 143785984 | tf_op jit(solution)/shard_map/jvp(bngqk,bknd->bqngd)/dot_general | solution.py:44
  765.0 23.8 %convolution_convert_fusion.1 = bf16[2,2048,4096]{2,1,0:T(8,128)(2,1)} fusion(bf16[2,2048,512]{1,2,0:T(8,128)(2,1)} %bitcast.244, bf16[512,4096]{1,0:T(8,128)(2,1)S(1)} %copy-done.26), kind=kOutput, calls=%fused_computation.22 | convolution fusion | flops 17196646400 | bytes 41943040 | tf_op jit(solution)/shard_map/bsk,kd->bsd/dot_general | solution.py:58
  788.8 0.1 reduce-scatter.3.cloned.1.call-update
  788.9 26.9 %bitcast_convert_fusion.1 = bf16[512,4096]{1,0:T(8,128)(2,1)} fusion(bf16[2,2048,512]{1,2,0:T(8,128)(2,1)} %bitcast.245, bf16[2,2048,4096]{2,1,0:T(8,128)(2,1)} %all-gather.5.cloned.1.call-done), kind=kOutput, calls=%fused_computation.46 | convolution fusion | flops 17181966336 | bytes 41943040 | tf_op jit(solution)/shard_map/bsk,bsd->kd/dot_general | solution.py:62
  815.8 34.0 %fusion.33 = bf16[4096,1,768]{2,0,1:T(8,128)(2,1)} fusion(bf16[2,2048,4096]{2,1,0:T(8,128)(2,1)} %all-gather.3.cloned.1.call-done, bf16[2,2048,768]{1,2,0:T(8,128)(2,1)} %bitcast.239, u8[2048,768]{0,1:T(8,128)(4,1)S(1)} %copy-done.9), kind=kOutput, calls=%fused_computation.57 | convolution fusion | flops 25788678144 | bytes 47710208 | tf_op jit(solution)/shard_map/bsd,bsnc->dnc/dot_general | solution.py:66
  849.8 0.0 copy-start.22
  849.8 32.3 %reduce-scatter.5.cloned.1.call-done = bf16[2,256,4096]{2,1,0:T(8,128)(2,1)} async-done(((bf16[2,2048,4096]{2,1,0:T(8,128)(2,1)}), bf16[2,256,4096]{2,1,0:T(8,128)(2,1)}) %reduce-scatter.5.cloned.1.call-update) | async-done | bytes 4194320 | tf_op jit(solution)/shard_map/reduce_scatter | solution.py:68
  882.1 5.4 fusion.28
  887.5 0.5 copy-done.2
  888.0 3.8 fusion.26
  891.8 25.1 %psum.7 = bf16[4096]{0:T(1024)(128)(2,1)} all-reduce(f32[4096]{0:T(1024)S(1)} %get-tuple-element.5), channel_id=1, replica_groups=mesh['dp'=2,'tp'=8] {'tp'}, use_global_device_ids=true, to_apply=%region_10.11 | all-reduce | flops 4096 | bytes 24576 | tf_op jit(solution)/shard_map/psum | solution.py:71
  916.9 133.9 %reduce-scatter.3.cloned.1.call-done = bf16[2,256,4096]{2,1,0:T(8,128)(2,1)} async-done(((bf16[2,2048,4096]{2,1,0:T(8,128)(2,1)}), bf16[2,256,4096]{2,1,0:T(8,128)(2,1)}) %reduce-scatter.3.cloned.1.call-update) | async-done | bytes 4194320 | tf_op jit(solution)/shard_map/reduce_scatter | solution.py:59
  1050.8 11.0 %add_convert_fusion = (bf16[2,256,4096]{2,1,0:T(8,128)(2,1)}, bf16[2,256,4096]{2,1,0:T(8,128)(2,1)}) fusion(bf16[2,256,4096]{2,1,0:T(8,128)(2,1)} %param.9, bf16[2,256,4096]{2,1,0:T(8,128)(2,1)} %param.5, bf16[2,256,4096]{2,1,0:T(8,128)(2,1)} %reduce-scatter.5.cloned.1.call-done, f32[2,256]{1,0:T(2,128)S(1)} %negate_multiply_fusion, ...), kind=kLoop, calls=%fused_computation.47 | loop fusion | flops 31457280 | bytes 25190400 | tf_op jit(solution)/shard_map/convert_element_type | solution.py:70
  (48 shorter events, 0.1 us)
Async XLA Ops:
  7.2 7.1 copy-start.25
  7.2 168.4 %all-gather.3.cloned.1.call-start = ((), (), s32[]{:S(2)}) async-start(), calls=%async_computation.2 | async-start | bytes 37748736 | tf_op jit(solution)/shard_map/all_gather | solution.py:54
  7.3 8.2 copy-start
  10.2 4.0 copy-start.18
  13.7 0.6 copy-start.23
  14.3 0.6 copy-start.21
  14.8 0.6 copy-start.14
  19.9 312.0 %all-gather.5.cloned.1.call-start = ((), (), s32[]{:S(2)}) async-start(), calls=%async_computation.4 | async-start | bytes 37748736 | tf_op jit(solution)/shard_map/all_gather | solution.py:61
  20.7 861.4 %reduce-scatter.5.cloned.1.call-start = ((), (), s32[]{:S(2)}) async-start(), calls=%async_computation.5 | async-start | bytes 37748736 | tf_op jit(solution)/shard_map/reduce_scatter | solution.py:68
  24.5 204.9 %copy-start.3 = (f32[2048,64]{1,0:T(8,128)}, f32[2048,64]{1,0:T(8,128)S(1)}, u32[]{:S(2)}) copy-start(f32[2048,64]{1,0:T(8,128)S(1)} %get-tuple-element.17) | copy-start | bytes 1572868
  24.5 204.9 %copy-start.5 = (f32[2048,64]{1,0:T(8,128)}, f32[2048,64]{1,0:T(8,128)S(1)}, u32[]{:S(2)}) copy-start(f32[2048,64]{1,0:T(8,128)S(1)} %get-tuple-element.18) | copy-start | bytes 1572868
  229.3 5.0 copy-start.11
  331.2 24.4 %copy-start.16 = (f32[2,4,2048]{2,1,0:T(4,128)}, f32[2,4,2048]{2,1,0:T(4,128)S(1)}, u32[]{:S(2)}) copy-start(f32[2,4,2048]{2,1,0:T(4,128)S(1)} %fusion.56) | copy-start | bytes 196612
  355.6 48.5 %copy-start.20 = (f32[2,4,2048]{2,1,0:T(4,128)S(1)}, f32[2,4,2048]{2,1,0:T(4,128)}, u32[]{:S(2)}) copy-start(f32[2,4,2048]{2,1,0:T(4,128)} %multiply_divide_fusion) | copy-start | bytes 196612
  404.1 78.2 %copy-start.17 = (f32[2,4,2048]{2,1,0:T(4,128)S(1)}, f32[2,4,2048]{2,1,0:T(4,128)}, u32[]{:S(2)}) copy-start(f32[2,4,2048]{2,1,0:T(4,128)} %copy-done.16) | copy-start | bytes 196612
  482.3 83.1 %copy-start.12 = (bf16[2,2048,64]{2,1,0:T(8,128)(2,1)S(1)}, bf16[2,2048,64]{2,1,0:T(8,128)(2,1)}, u32[]{:S(2)}) copy-start(bf16[2,2048,64]{2,1,0:T(8,128)(2,1)} %copy-done.11) | copy-start | bytes 1572868
  482.3 83.1 %copy-start.13 = (bf16[2,2048,64]{2,1,0:T(8,128)(2,1)S(1)}, bf16[2,2048,64]{2,1,0:T(8,128)(2,1)}, u32[]{:S(2)}) copy-start(bf16[2,2048,64]{2,1,0:T(8,128)(2,1)} %get-tuple-element.16) | copy-start | bytes 1572868
  645.3 7.7 copy-start.4
  645.3 7.7 copy-start.6
  645.3 7.7 copy-start.7
  665.6 2.4 copy-start.10
  671.0 8.9 copy-start.8
  714.6 336.2 %reduce-scatter.3.cloned.1.call-start = ((), (), s32[]{:S(2)}) async-start(), calls=%async_computation.3 | async-start | bytes 37748736 | tf_op jit(solution)/shard_map/reduce_scatter | solution.py:59
  714.7 50.3 %copy-start.26 = (bf16[512,4096]{1,0:T(8,128)(2,1)S(1)}, bf16[512,4096]{1,0:T(8,128)(2,1)}, u32[]{:S(2)}) copy-start(bf16[512,4096]{1,0:T(8,128)(2,1)} %param.8) | copy-start | bytes 12582916
  788.9 26.9 %copy-start.9 = (u8[2048,768]{0,1:T(8,128)(4,1)S(1)}, u8[2048,768]{0,1:T(8,128)(4,1)}, u32[]{:S(2)}) copy-start(u8[2048,768]{0,1:T(8,128)(4,1)} %fusion.53) | copy-start | bytes 4718596
  815.8 66.3 %copy-start.15 = (f32[4096]{0:T(1024)S(1)}, f32[4096]{0:T(1024)}, u32[]{:S(2)}) copy-start(f32[4096]{0:T(1024)} %copy-done.14) | copy-start | bytes 49156
  815.8 66.3 %copy-start.19 = (f32[2,256]{1,0:T(2,128)S(1)}, f32[2,256]{1,0:T(2,128)}, u32[]{:S(2)}) copy-start(f32[2,256]{1,0:T(2,128)} %copy-done.18) | copy-start | bytes 6148
  849.8 37.7 %copy-start.24 = (f32[2,256]{1,0:T(2,128)S(1)}, f32[2,256]{1,0:T(2,128)}, u32[]{:S(2)}) copy-start(f32[2,256]{1,0:T(2,128)} %copy-done.23) | copy-start | bytes 6148
  849.8 37.7 %copy-start.22 = (f32[2,256]{1,0:T(2,128)S(1)}, f32[2,256]{1,0:T(2,128)}, u32[]{:S(2)}) copy-start(f32[2,256]{1,0:T(2,128)} %copy-done.21) | copy-start | bytes 6148
  882.1 5.4 copy-start.1
  882.1 5.9 copy-start.2
Sparse Core Ops, SparseCore 0:
  20.0 155.5 all-gather.2
  177.2 153.5 all-gather.4
  714.7 167.2 reduce-scatter.4
  884.3 166.4 reduce-scatter.2
where the time goes:
time: 1080 us; the launch traced here: 1070 us
  matrix products  572 us (53%)
  waiting for transfers between devices  314 us (29%)
  other arithmetic  117 us (11%)
  local copies, waits for them, and re-layouts  26.2 us (2%)
  blocking collectives  25.1 us (2%)
  between operations  14.6 us (1%)
    dot_general x3, matrix products, attention_core(): jnp.einsum('bqngd,bknd->bngqk', query_rot, key_rot, preferred_element_typ...  217 us
    dot_general x3, matrix products, attention_core(): jnp.einsum('bngqk,bknd->bqngd', attn_prob, val_head, preferred_element_ty...  177 us
    all_gather x1, waiting for transfers between devices, device_step(): h_full = lax.all_gather(h_loc, 'tp', axis=1, tiled=True)  147 us
    reduce_scatter x1, waiting for transfers between devices, device_step(): out_loc = lax.psum_scatter(out_part, 'tp', scatter_dimension=1, tiled=True)  134 us
    reduce_sum x1, other arithmetic, attention_core(): attn_prob = jax.nn.softmax(scores, axis=-1).astype(jnp.bfloat16)  42.4 us
    dot_general x1, matrix products, device_step(): jnp.einsum('bsnc,dnc->bsd', d_qkv, w_qkv, preferred_element_type=jnp.floa...  34.6 us
    dot_general x1, matrix products, device_step(): jnp.einsum('bsd,dnc->bsnc', h_full, w_qkv, preferred_element_type=jnp.flo...  34.2 us
    dot_general x1, matrix products, device_step(): jnp.einsum('bsd,bsnc->dnc', h_full, d_qkv, preferred_element_type=jnp.flo...  34 us
  transfers between devices with their start and end apart: 4, of which 3 were waited for; matrix products, arithmetic and copies ran while one was open for 29% of the time, Pallas kernels for 0%

commit v1 on v0

v1 whole, which is shorter than its diff:
```python
import functools
import jax
import jax.numpy as jnp
from jax import lax
from jax.experimental import pallas as pl
from jax.experimental.pallas import tpu as pltpu
from jax.sharding import PartitionSpec as P

CLIP_QKV = 8.0
ROPE_THETA = 500000.0
LN_EPS = 1e-5
LOG2E = 1.4426950408889634
HD = 128
F32 = jnp.float32
BF16 = jnp.bfloat16
NT = (((1,), (1,)), ((), ()))


def layer_norm(x_f32, gain_f32):
    row_mean = jnp.mean(x_f32, axis=-1, keepdims=True)
    centered = x_f32 - row_mean
    variance = jnp.mean(centered * centered, axis=-1, keepdims=True)
    return (centered * lax.rsqrt(variance + LN_EPS) * gain_f32).astype(BF16)


def rope_tables(seq_len):
    inv_freq = 1.0 / (ROPE_THETA ** (jnp.arange(0, HD, 2, dtype=F32) / HD))
    angles = jnp.arange(seq_len, dtype=F32)[:, None] * inv_freq[None, :]
    cos_t, sin_t = jnp.cos(angles), jnp.sin(angles)
    return jnp.concatenate([cos_t, cos_t], -1), jnp.concatenate([-sin_t, sin_t], -1)


def rope(v, cos2, sin2):
    return v * cos2 + pltpu.roll(v, HD // 2, 1) * sin2


def rope_t(v, cos2, sin2):
    return v * cos2 - pltpu.roll(v, HD // 2, 1) * sin2


def causal_mask(bk, bq):
    key_i = lax.broadcasted_iota(jnp.int32, (bk, bq), 0)
    query_i = lax.broadcasted_iota(jnp.int32, (bk, bq), 1)
    return key_i <= query_i


def attn_fwd_kernel(scale, blk, q_ref, k_ref, v_ref, cos_ref, sin_ref, o_ref, lse_ref, k_s, vt_s):
    head, qi = pl.program_id(0), pl.program_id(1)
    nblk = k_s.shape[0]

    @pl.when((head == 0) & (qi == 0))
    def _():
        for n in range(nblk):
            rows = pl.ds(n * blk, blk)
            k_s[n] = rope(k_ref[rows, :].astype(F32), cos_ref[rows, :], sin_ref[rows, :]).astype(BF16)
            vt_s[n] = v_ref[rows, :].T

    rows = pl.ds(pl.multiple_of(qi * blk, blk), blk)
    q = rope(q_ref[...].astype(F32), cos_ref[rows, :], sin_ref[rows, :]).astype(BF16)

    def block(j, carry, masked):
        m_old, l_old, acc = carry
        s = lax.dot_general(k_s[j], q, NT, preferred_element_type=F32) * (scale * LOG2E)
        if masked:
            s = jnp.where(causal_mask(blk, blk), s, -1e30)
        m_new = jnp.maximum(m_old, jnp.max(s, axis=0, keepdims=True))
        p = jnp.exp2(s - m_new)
        alpha = jnp.exp2(m_old - m_new)
        l_new = alpha * l_old + jnp.sum(p, axis=0, keepdims=True)
        pv = jnp.dot(vt_s[j], p.astype(BF16), preferred_element_type=F32)
        return m_new, l_new, acc * alpha + pv

    init = (jnp.full((1, blk), -1e30, F32), jnp.zeros((1, blk), F32), jnp.zeros((HD, blk), F32))
    carry = block(qi, init, True)
    m, l, acc = lax.fori_loop(0, qi, lambda j, c: block(j, c, False), carry)
    o_ref[...] = (acc / l).T.astype(BF16)
    lse_ref[0, 0] = m + jnp.log2(l)


def attn_fwd(qkv, cos2, sin2, blk=512):
    seq, width = qkv.shape
    groups = width // HD - 2
    nblk = seq // blk
    flops = 4 * groups * seq * seq * HD
    whole = lambda c: pl.BlockSpec((seq, HD), lambda h, i: (0, c))
    return pl.pallas_call(
        functools.partial(attn_fwd_kernel, HD ** -0.5, blk),
        grid=(groups, nblk),
        in_specs=[pl.BlockSpec((blk, HD), lambda h, i: (i, h)), whole(groups), whole(groups + 1), whole(0), whole(0)],
        out_specs=[pl.BlockSpec((blk, HD), lambda h, i: (i, h)),
                   pl.BlockSpec((1, 1, 1, blk), lambda h, i: (h, i, 0, 0))],
        out_shape=[jax.ShapeDtypeStruct((seq, groups * HD), BF16),
                   jax.ShapeDtypeStruct((groups, nblk, 1, blk), F32)],
        scratch_shapes=[pltpu.VMEM((nblk, blk, HD), BF16), pltpu.VMEM((nblk, HD, blk), BF16)],
        compiler_params=pltpu.CompilerParams(dimension_semantics=("arbitrary", "arbitrary"),
                                             vmem_limit_bytes=40 * 1024 * 1024),
        cost_estimate=pl.CostEstimate(flops=flops * 3, bytes_accessed=6 << 20, transcendentals=0),
        name="attn_fwd",
    )(qkv, qkv, qkv, cos2, sin2)


def attn_bwd_kernel(scale, blk, groups, q_ref, k_ref, v_ref, do_ref, o_ref, lse_ref, cos_ref, sin_ref,
                    out_ref, k_s, kt_s, dk_s, dv_s):
    head = pl.program_id(0)
    nblk = k_s.shape[0]

    @pl.when(head == 0)
    def _():
        for n in range(nblk):
            rows = pl.ds(n * blk, blk)
            kr = rope(k_ref[rows, :].astype(F32), cos_ref[rows, :], sin_ref[rows, :])
            k_s[n] = kr.astype(BF16)
            kt_s[n] = kr.T.astype(BF16)
        dk_s[...] = jnp.zeros_like(dk_s)
        dv_s[...] = jnp.zeros_like(dv_s)

    def passes(raw, grad):
        return jnp.where(jnp.abs(raw.astype(F32)) < CLIP_QKV, grad, 0.0).astype(BF16)

    def q_block(qi, _):
        rows = pl.ds(pl.multiple_of(qi * blk, blk), blk)
        cos2, sin2 = cos_ref[rows, :], sin_ref[rows, :]
        q_raw = q_ref[rows, :]
        q = rope(q_raw.astype(F32), cos2, sin2).astype(BF16)
        do = do_ref[rows, :]
        delta = jnp.sum((do.astype(F32) * o_ref[rows, :].astype(F32)).T, axis=0, keepdims=True)
        lse = lse_ref[0, qi]

        def block(j, dq_t, masked):
            keys = pl.ds(pl.multiple_of(j * blk, blk), blk)
            s = lax.dot_general(k_s[j], q, NT, preferred_element_type=F32) * (scale * LOG2E)
            p = jnp.exp2(s - lse)
            if masked:
                p = jnp.where(causal_mask(blk, blk), p, 0.0)
            dp = lax.dot_general(v_ref[keys, :], do, NT, preferred_element_type=F32)
            dp = dp.astype(BF16).astype(F32)
            ds = (p * (dp - delta)).astype(BF16)
            dv_s[j] += jnp.dot(p.astype(BF16), do, preferred_element_type=F32)
            dk_s[j] += jnp.dot(ds, q, preferred_element_type=F32)
            return dq_t + jnp.dot(kt_s[j], ds, preferred_element_type=F32)

        dq_t = block(qi, jnp.zeros((HD, blk), F32), True)
        dq_t = lax.fori_loop(0, qi, lambda j, c: block(j, c, False), dq_t)
        dq = (dq_t.T * scale).astype(BF16).astype(F32)
        dq = rope_t(dq, cos2, sin2)
        out_ref[rows, pl.ds(pl.multiple_of(head * HD, HD), HD)] = passes(q_raw, dq)
        return 0

    lax.fori_loop(0, nblk, q_block, 0)

    @pl.when(head == groups - 1)
    def _():
        for n in range(nblk):
            rows = pl.ds(n * blk, blk)
            dk = (dk_s[n] * scale).astype(BF16).astype(F32)
            dk = rope_t(dk, cos_ref[rows, :], sin_ref[rows, :])
            out_ref[rows, groups * HD:(groups + 1) * HD] = passes(k_ref[rows, :], dk)
            out_ref[rows, (groups + 1) * HD:] = passes(v_ref[rows, :], dv_s[n])


def attn_bwd(qkv, d_attn, attn, lse, cos2, sin2):
    seq, width = qkv.shape
    groups = width // HD - 2
    nblk, blk = lse.shape[1], lse.shape[3]
    flops = 10 * groups * seq * seq * HD
    whole = lambda c: pl.BlockSpec((seq, HD), lambda h: (0, c))
    per_head = pl.BlockSpec((seq, HD), lambda h: (0, h))
    return pl.pallas_call(
        functools.partial(attn_bwd_kernel, HD ** -0.5, blk, groups),
        grid=(groups,),
        in_specs=[per_head, whole(groups), whole(groups + 1), per_head, per_head,
                  pl.BlockSpec((1, nblk, 1, blk), lambda h: (h, 0, 0, 0)), whole(0), whole(0)],
        out_specs=pl.BlockSpec((seq, width), lambda h: (0, 0)),
        out_shape=jax.ShapeDtypeStruct((seq, width), BF16),
        scratch_shapes=[pltpu.VMEM((nblk, blk, HD), BF16), pltpu.VMEM((nblk, HD, blk), BF16),
                        pltpu.VMEM((nblk, blk, HD), F32), pltpu.VMEM((nblk, blk, HD), F32)],
        compiler_params=pltpu.CompilerParams(dimension_semantics=("arbitrary",), vmem_limit_bytes=40 * 1024 * 1024),
        cost_estimate=pl.CostEstimate(flops=flops * 3, bytes_accessed=12 << 20, transcendentals=0),
        name="attn_bwd",
    )(qkv, qkv, qkv, d_attn, attn, lse, cos2, sin2)


def norm_bwd_kernel(x_ref, gain_ref, dh_ref, dy_ref, *refs):
    dx_ref, dg_ref = refs[-2:]
    x = x_ref[0].astype(F32)
    mean = jnp.mean(x, axis=-1, keepdims=True)
    centered = x - mean
    rstd = lax.rsqrt(jnp.mean(centered * centered, axis=-1, keepdims=True) + LN_EPS)
    xhat = centered * rstd
    dh = dh_ref[...].astype(F32)
    part = jnp.sum(dh * xhat, axis=0, keepdims=True)

    @pl.when(pl.program_id(0) == 0)
    def _():
        dg_ref[...] = jnp.zeros_like(dg_ref)

    dg_ref[...] += part
    dxh = dh * gain_ref[...]
    m1 = jnp.mean(dxh, axis=-1, keepdims=True)
    m2 = jnp.mean(dxh * xhat, axis=-1, keepdims=True)
    dx_ref[0] = (dy_ref[0].astype(F32) + rstd * (dxh - m1 - xhat * m2)).astype(BF16)


def norm_bwd(b, x, gain, dh, dy, prev, blk=64):
    rows, width = dh.shape
    seq_spec = pl.BlockSpec((1, blk, width), lambda i: (b, i, 0))
    row_spec = pl.BlockSpec((blk, width), lambda i: (i, 0))
    vec_spec = pl.BlockSpec((1, width), lambda i: (0, 0))
    kept = [] if prev is None else [prev]
    return pl.pallas_call(
        norm_bwd_kernel,
        grid=(rows // blk,),
        in_specs=[seq_spec, vec_spec, row_spec, seq_spec] + [pl.BlockSpec(memory_space=pl.ANY) for _ in kept],
        out_specs=[seq_spec, vec_spec],
        out_shape=[jax.ShapeDtypeStruct(x.shape, BF16), jax.ShapeDtypeStruct((1, width), F32)],
        input_output_aliases={4: 0} if kept else {},
        compiler_params=pltpu.CompilerParams(dimension_semantics=("arbitrary",), vmem_limit_bytes=32 * 1024 * 1024),
        cost_estimate=pl.CostEstimate(flops=rows * width * 40, bytes_accessed=rows * width * 8, transcendentals=0),
        name="norm_bwd",
    )(x, gain, dh, dy, *kept)


def residual_kernel(x_ref, o_ref, *refs):
    refs[-1][0] = (x_ref[0].astype(F32) + o_ref[...].astype(F32)).astype(BF16)


def residual(b, x, out, prev, blk=64):
    rows, width = out.shape
    seq_spec = pl.BlockSpec((1, blk, width), lambda i: (b, i, 0))
    row_spec = pl.BlockSpec((blk, width), lambda i: (i, 0))
    kept = [] if prev is None else [prev]
    return pl.pallas_call(
        residual_kernel,
        grid=(rows // blk,),
        in_specs=[seq_spec, row_spec] + [pl.BlockSpec(memory_space=pl.ANY) for _ in kept],
        out_specs=seq_spec,
        out_shape=jax.ShapeDtypeStruct(x.shape, BF16),
        input_output_aliases={2: 0} if kept else {},
        compiler_params=pltpu.CompilerParams(dimension_semantics=("arbitrary",), vmem_limit_bytes=32 * 1024 * 1024),
        cost_estimate=pl.CostEstimate(flops=rows * width * 4, bytes_accessed=rows * width * 6, transcendentals=0),
        name="residual",
    )(x, out, *kept)


def mm(a, b, dims, dtype=BF16):
    return lax.dot_general(a, b, (dims, ((), ())), preferred_element_type=F32).astype(dtype)


def solution(mesh):
    def device_step(x_seq, ln_gain, w_qkv, w_out, y_grad):
        batch = x_seq.shape[0]
        d_model, kv_loc, slot = w_qkv.shape
        w_in = w_qkv.reshape(d_model, kv_loc * slot)
        gain = ln_gain.astype(F32)

        def gather(v):
            return lax.all_gather(v, 'tp', axis=0, tiled=True)

        def scatter(v):
            return lax.psum_scatter(v, 'tp', scatter_dimension=0, tiled=True)

        after = lambda v, *first: lax.optimization_barrier((v,) + first)[0]
        dy_loc = [y_grad[b] for b in range(batch)]
        x_in = after(x_seq, *dy_loc)
        h_loc = layer_norm(x_in.astype(F32), gain)
        dy0 = gather(dy_loc[0])
        h0 = gather(h_loc[0])
        h1 = gather(h_loc[1])
        dy1 = gather(dy_loc[1])
        cos2, sin2 = rope_tables(h0.shape[0])

        def forward(h):
            raw = mm(h, w_in, ((1,), (0,)))
            qkv = jnp.minimum(jnp.maximum(raw, -CLIP_QKV), CLIP_QKV)
            return (qkv,) + tuple(attn_fwd(qkv, cos2, sin2))

        def backward(dy, qkv, attn, lse):
            d_attn = mm(dy, w_out, ((1,), (1,)))
            d_qkv = attn_bwd(qkv, d_attn, attn, lse, cos2, sin2)
            return d_qkv, mm(d_qkv, w_in, ((1,), (1,)))

        qkv0, attn0, lse0 = forward(h0)
        out0 = mm(attn0, w_out, ((1,), (0,)))
        out_loc0 = scatter(out0)
        dqkv0, dh0 = backward(after(dy0, out0), qkv0, attn0, lse0)
        dh_loc0 = scatter(dh0)
        qkv1, attn1, lse1 = forward(after(h1, dh0))
        dqkv1, dh1 = backward(dy1, qkv1, attn1, lse1)
        dh_loc1 = scatter(dh1)
        out1 = mm(after(attn1, dh1), w_out, ((1,), (0,)))
        out_loc1 = scatter(out1)
        wout_grad = (mm(after(attn0, out1), dy0, ((0,), (0,)), F32) + mm(attn1, dy1, ((0,), (0,)), F32)).astype(BF16)
        wqkv_grad = (mm(h0, after(dqkv0, out1), ((0,), (0,)), F32) + mm(h1, dqkv1, ((0,), (0,)), F32)).astype(BF16)
        y_out = residual(1, x_seq, out_loc1, residual(0, x_seq, out_loc0, None))
        g_row = gain[None, :]
        dx, part0 = norm_bwd(0, x_seq, g_row, dh_loc0, y_grad, None)
        x_grad, part1 = norm_bwd(1, x_seq, g_row, dh_loc1, y_grad, dx)
        gain_grad = lax.psum((part0 + part1)[0], 'tp').astype(BF16)
        return y_out, x_grad, gain_grad, wqkv_grad.reshape(w_qkv.shape), wout_grad

    specs_in = (P('dp', 'tp', None), P(None), P(None, 'tp', None), P('tp', None), P('dp', 'tp', None))
    specs_out = (P('dp', 'tp', None), P('dp', 'tp', None), P('dp'), P('dp', 'tp', None), P(('dp', 'tp'), None))

    return jax.shard_map(device_step, mesh=mesh, in_specs=specs_in, out_specs=specs_out, check_vma=False)
```

time: 1080 us -> 731 us (0.68)
  matrix products: 572 us -> 204 us
  Pallas kernels: 0 us -> 156 us
  other arithmetic: 117 us -> 11 us
  waiting for transfers between devices: 314 us -> 275 us
    dot_general x12, matrix products: 572 us -> 204 us  [mm(): lax.dot_general(a, b, (dims, ((), ())), preferred_element_type=F32)]
    pallas_call x0 -> x8, Pallas kernels: none -> 156 us  [the longest x2 80.1 us: attn_bwd(): pl.pallas_call(functools.partial(attn_bwd_kernel, HD ** (-0.5), blk, grou...]
    reduce_sum x3 -> x0, other arithmetic: 51.5 us -> none  [the longest x1 42.4 us: attention_core(): attn_prob = jax.nn.softmax(scores, axis=-1).astype(jnp.bfloat16)]
    reduce_scatter x2 -> x4, waiting for transfers between devices: 166 us -> 137 us  [scatter(): return lax.psum_scatter(v, 'tp', scatter_dimension=0, tiled=True)]
    unnamed x56 -> x58, local copies, waits for them, and re-layouts: 10.1 us -> 28.6 us
    convert_element_type x7 -> x2, other arithmetic: 20.6 us -> 2.31 us  [the longest x1 2.3 us: layer_norm(): return (centered * lax.rsqrt(variance + LN_EPS) * gain_f32).astype(BF16)]
    add_any x3 -> x0, other arithmetic: 12.8 us -> none  [the longest x2 9.8 us: rotate(): half_hi * sin_t]
    all_gather x2 -> x4, waiting for transfers between devices: 147 us -> 136 us  [gather(): return lax.all_gather(v, 'tp', axis=0, tiled=True)]
  transfers between devices with their start and end apart: 4 -> 8, of which waited for: 3 -> 7; matrix products, arithmetic and copies ran while one was open for 29% -> 30% of each run, Pallas kernels for 0% -> 21%
where the time goes in v1:
time: 731 us; the launch traced here: 723 us
  waiting for transfers between devices  275 us (38%)
  matrix products  204 us (28%)
  Pallas kernels  156 us (21%)
  local copies, waits for them, and re-layouts  35.9 us (5%)
  blocking collectives  25.5 us (3%)
  between operations  14.7 us (2%)
  other arithmetic  11 us (2%)
    dot_general x12, matrix products, mm(): lax.dot_general(a, b, (dims, ((), ())), preferred_element_type=F32)  204 us
    reduce_scatter x4, waiting for transfers between devices, scatter(): return lax.psum_scatter(v, 'tp', scatter_dimension=0, tiled=True)  137 us
    all_gather x4, waiting for transfers between devices, gather(): return lax.all_gather(v, 'tp', axis=0, tiled=True)  136 us
    pallas_call x2, Pallas kernels, attn_bwd(): pl.pallas_call(functools.partial(attn_bwd_kernel, HD ** (-0.5), blk, grou...  80.1 us
    pallas_call x2, Pallas kernels, attn_fwd(): pl.pallas_call(functools.partial(attn_fwd_kernel, HD ** (-0.5), blk), gri...  60.7 us
    unnamed x58, local copies, waits for them, and re-layouts  28.6 us
    psum x1, blocking collectives, device_step(): gain_grad = lax.psum((part0 + part1)[0], 'tp').astype(BF16)  25.5 us
  transfers between devices with their start and end apart: 8, of which 7 were waited for; matrix products, arithmetic and copies ran while one was open for 30% of the time, Pallas kernels for 21%

profile of v1, /device:TPU:112, one launch (start us, length us, event | category | flops | bytes accessed | tf_op | source)
XLA Modules:
  0.0 723.4 jit_solution(5336393151172830708)
XLA Ops:
  7.2 0.1 all-gather.11.cloned.1.call-start
  7.3 3.0 convert_reduce_fusion
  10.2 0.5 copy-done
  10.7 1.2 fusion.10
  12.0 2.3 fusion.12
  14.3 2.5 fusion.49
  16.8 0.1 all-gather.11.cloned.1.call-update
  16.9 0.1 all-gather.13.cloned.1.call-start
  16.9 4.7 fusion.48
  21.7 0.1 all-gather.9.cloned.1.call-start
  21.8 0.7 all-gather.9.cloned.1.call-update
  22.5 0.1 all-gather.15.cloned.1.call-start
  22.6 0.6 all-gather.15.cloned.1.call-update
  23.2 0.1 reduce-scatter.11.cloned.1.call-start
  23.2 3.9 fusion.44
  27.1 0.6 pad_maximum_fusion
  27.8 73.0 %all-gather.11.cloned.1.call-done = bf16[1,2048,4096]{2,1,0:T(8,128)(2,1)} async-done(((bf16[1,256,4096]{2,1,0:T(8,128)(2,1)}), bf16[1,2048,4096]{2,1,0:T(8,128)(2,1)}) %all-gather.11.cloned.1.call-update) | async-done | bytes 16777232 | tf_op jit(solution)/shard_map/all_gather | solution.py:257
  100.7 18.2 %fusion.34.q_ref.k_ref.v_ref = bf16[2048,768]{1,0:T(8,128)(2,1)S(1)} fusion(bf16[4096,1,768]{2,0,1:T(8,128)(2,1)} %param.7, bf16[1,2048,4096]{2,1,0:T(8,128)(2,1)} %all-gather.11.cloned.1.call-done), kind=kOutput, calls=%fused_computation.30 | convolution fusion | flops 12888047616 | bytes 26214400 | tf_op jit(solution)/shard_map/dot_general | solution.py:246
  119.0 30.4 %attn_fwd.2 = (bf16[2048,512]{1,0:T(8,128)(2,1)S(1)}, f32[4,4,1,512]{3,2,1,0:T(1,128)S(1)}) custom-call(bf16[2048,768]{1,0:T(8,128)(2,1)S(1)} %fusion.34.q_ref.k_ref.v_ref, bf16[2048,768]{1,0:T(8,128)(2,1)S(1)} %fusion.34.q_ref.k_ref.v_ref, bf16[2048,768]{1,0:T(8,128)(2,1)S(1)} %fusion.34.q_ref.k_ref.v_ref, f32[2048,128]{1,0:T(8,128)S(1)} %get-tuple-element.40.cos_ref, ...), custom_call_target="tpu_custom_call" | custom-call | flops 25769803776 | bytes 6291456 | tf_op jit(solution)/shard_map/attn_fwd/pallas_call | solution.py:86
  149.4 11.7 %convolution_convert_fusion.3 = bf16[2048,4096]{1,0:T(8,128)(2,1)} fusion(bf16[2048,512]{1,0:T(8,128)(2,1)S(1)} %get-tuple-element.32.o_ref, bf16[512,4096]{1,0:T(8,128)(2,1)S(1)} %copy-done.28), kind=kOutput, calls=%fused_computation.11 | convolution fusion | flops 8598323200 | bytes 23068672 | tf_op jit(solution)/shard_map/dot_general | solution.py:246
  161.0 1.4 copy-done.13
  162.4 21.9 %all-gather.13.cloned.1.call-done = bf16[1,2048,4096]{2,1,0:T(8,128)(2,1)} async-done(((bf16[1,256,4096]{2,1,0:T(8,128)(2,1)}), bf16[1,2048,4096]{2,1,0:T(8,128)(2,1)}) %all-gather.13.cloned.1.call-update) | async-done | bytes 16777232 | tf_op jit(solution)/shard_map/all_gather | solution.py:257
  184.3 13.8 %convolution_convert_fusion.4.do_ref = bf16[2048,512]{1,0:T(8,128)(2,1)S(1)} fusion(bf16[2048,4096]{1,0:T(8,128)(2,1)} %bitcast.64, bf16[512,4096]{1,0:T(8,128)(2,1)} %param.8), kind=kOutput, calls=%fused_computation.32 | convolution fusion | flops 8590983168 | bytes 23068672 | tf_op jit(solution)/shard_map/dot_general | solution.py:246
  198.1 40.0 %attn_bwd.2 = bf16[2048,768]{1,0:T(8,128)(2,1)S(1)} custom-call(bf16[2048,768]{1,0:T(8,128)(2,1)S(1)} %copy-done.24, bf16[2048,768]{1,0:T(8,128)(2,1)S(1)} %copy-done.24, bf16[2048,768]{1,0:T(8,128)(2,1)S(1)} %copy-done.24, bf16[2048,512]{1,0:T(8,128)(2,1)S(1)} %convolution_convert_fusion.4.do_ref, bf16[2048,512]{1,0:T(8,128)(2,1)S(1)} %copy-done.14, ...), custom_call_target="tpu_custom_call" | custom-call | flops 64424509440 | bytes 12582912 | tf_op jit(solution)/shard_map/attn_bwd/pallas_call | solution.py:168
  238.1 1.7 copy-done.19
  239.8 18.7 %convolution_convert_fusion.2 = bf16[2048,4096]{1,0:T(8,128)(2,1)} fusion(bf16[2048,768]{1,0:T(8,128)(2,1)S(1)} %attn_bwd.2, bf16[4096,1,768]{2,0,1:T(8,128)(2,1)} %param.7), kind=kOutput, calls=%fused_computation.10 | convolution fusion | flops 12893290496 | bytes 26214400 | tf_op jit(solution)/shard_map/dot_general | solution.py:246
  258.6 0.1 reduce-scatter.9.cloned.1.call-start
  258.6 9.3 %all-gather.9.cloned.1.call-done = bf16[1,2048,4096]{2,1,0:T(8,128)(2,1)} async-done(((bf16[1,256,4096]{2,1,0:T(8,128)(2,1)}), bf16[1,2048,4096]{2,1,0:T(8,128)(2,1)}) %all-gather.9.cloned.1.call-update) | async-done | bytes 16777232 | tf_op jit(solution)/shard_map/all_gather | solution.py:257
  267.9 18.0 %fusion.26.q_ref.k_ref.v_ref = bf16[2048,768]{1,0:T(8,128)(2,1)S(1)} fusion(bf16[2048,4096]{1,0:T(8,128)(2,1)} %bitcast.65, bf16[4096,1,768]{2,0,1:T(8,128)(2,1)} %param.7), kind=kOutput, calls=%fused_computation.28 | convolution fusion | flops 12888047616 | bytes 26214400 | tf_op jit(solution)/shard_map/dot_general | solution.py:246
  286.0 30.4 %attn_fwd.3 = (bf16[2048,512]{1,0:T(8,128)(2,1)S(1)}, f32[4,4,1,512]{3,2,1,0:T(1,128)S(1)}) custom-call(bf16[2048,768]{1,0:T(8,128)(2,1)S(1)} %fusion.26.q_ref.k_ref.v_ref, bf16[2048,768]{1,0:T(8,128)(2,1)S(1)} %fusion.26.q_ref.k_ref.v_ref, bf16[2048,768]{1,0:T(8,128)(2,1)S(1)} %fusion.26.q_ref.k_ref.v_ref, f32[2048,128]{1,0:T(8,128)S(1)} %get-tuple-element.40.cos_ref, ...), custom_call_target="tpu_custom_call" | custom-call | flops 25769803776 | bytes 6291456 | tf_op jit(solution)/shard_map/attn_fwd/pallas_call | solution.py:86
  316.4 1.3 copy-done.16
  317.7 1.7 copy-done.25
  319.4 31.5 %all-gather.15.cloned.1.call-done = bf16[1,2048,4096]{2,1,0:T(8,128)(2,1)} async-done(((bf16[1,256,4096]{2,1,0:T(8,128)(2,1)}), bf16[1,2048,4096]{2,1,0:T(8,128)(2,1)}) %all-gather.15.cloned.1.call-update) | async-done | bytes 16777232 | tf_op jit(solution)/shard_map/all_gather | solution.py:257
  350.8 13.8 %fusion.39.do_ref = bf16[2048,512]{1,0:T(8,128)(2,1)S(1)} fusion(bf16[512,4096]{1,0:T(8,128)(2,1)} %param.8, bf16[1,2048,4096]{2,1,0:T(8,128)(2,1)} %all-gather.15.cloned.1.call-done), kind=kOutput, calls=%fused_computation.31 | convolution fusion | flops 8590983168 | bytes 23068672 | tf_op jit(solution)/shard_map/dot_general | solution.py:246
  364.6 40.2 %attn_bwd.3 = bf16[2048,768]{1,0:T(8,128)(2,1)S(1)} custom-call(bf16[2048,768]{1,0:T(8,128)(2,1)S(1)} %copy-done.26, bf16[2048,768]{1,0:T(8,128)(2,1)S(1)} %copy-done.26, bf16[2048,768]{1,0:T(8,128)(2,1)S(1)} %copy-done.26, bf16[2048,512]{1,0:T(8,128)(2,1)S(1)} %fusion.39.do_ref, bf16[2048,512]{1,0:T(8,128)(2,1)S(1)} %copy-done.17, ...), custom_call_target="tpu_custom_call" | custom-call | flops 64424509440 | bytes 12582912 | tf_op jit(solution)/shard_map/attn_bwd/pallas_call | solution.py:168
  404.8 1.7 copy-done.21
  406.5 18.7 %convolution_convert_fusion.1 = bf16[2048,4096]{1,0:T(8,128)(2,1)} fusion(bf16[2048,768]{1,0:T(8,128)(2,1)S(1)} %attn_bwd.3, bf16[4096,1,768]{2,0,1:T(8,128)(2,1)} %param.7), kind=kOutput, calls=%fused_computation.9 | convolution fusion | flops 12893290496 | bytes 26214400 | tf_op jit(solution)/shard_map/dot_general | solution.py:246
  425.3 0.1 reduce-scatter.7.cloned.1.call-start
  425.3 0.7 reduce-scatter.7.cloned.1.call-update
  426.1 0.1 reduce-scatter.5.cloned.1.call-start
  426.2 0.8 copy-done.18
  426.9 14.1 %convolution_convert_fusion = bf16[2048,4096]{1,0:T(8,128)(2,1)} fusion(bf16[2048,512]{1,0:T(8,128)(2,1)S(1)} %copy-done.18, bf16[512,4096]{1,0:T(8,128)(2,1)} %param.8), kind=kOutput, calls=%fused_computation.8 | convolution fusion | flops 8598323200 | bytes 23068672 | tf_op jit(solution)/shard_map/dot_general | solution.py:246
  441.1 14.7 %fusion = f32[512,4096]{1,0:T(8,128)} fusion(bf16[2048,512]{1,0:T(8,128)(2,1)S(1)} %copy-done.18, bf16[1,2048,4096]{2,1,0:T(8,128)(2,1)} %all-gather.15.cloned.1.call-done), kind=kOutput, calls=%fused_computation | convolution fusion | flops 8589934592 | bytes 27262976 | tf_op jit(solution)/shard_map/dot_general | solution.py:246
  455.8 17.5 %add_convert_fusion.1 = bf16[512,4096]{1,0:T(8,128)(2,1)} fusion(f32[512,4096]{1,0:T(8,128)} %fusion, bf16[2048,512]{1,0:T(8,128)(2,1)S(1)} %copy-done.15, bf16[1,2048,4096]{2,1,0:T(8,128)(2,1)} %all-gather.13.cloned.1.call-done), kind=kOutput, calls=%fused_computation.20 | convolution fusion | flops 8594128896 | bytes 31457280 | tf_op jit(solution)/shard_map/dot_general | solution.py:246
  473.3 20.3 %fusion.46 = f32[4096,768]{1,0:T(8,128)} fusion(bf16[2048,768]{1,0:T(8,128)(2,1)S(1)} %copy-done.22, bf16[1,2048,4096]{2,1,0:T(8,128)(2,1)} %all-gather.9.cloned.1.call-done), kind=kOutput, calls=%fused_computation.43 | convolution fusion | flops 12884901888 | bytes 32505856 | tf_op jit(solution)/shard_map/dot_general | solution.py:246
  493.6 24.8 %fusion.20 = bf16[4096,1,768]{2,0,1:T(8,128)(2,1)} fusion(f32[4096,768]{1,0:T(8,128)} %fusion.46, bf16[2048,768]{1,0:T(8,128)(2,1)S(1)} %copy-done.20, bf16[1,2048,4096]{2,1,0:T(8,128)(2,1)} %all-gather.11.cloned.1.call-done), kind=kOutput, calls=%fused_computation.26 | convolution fusion | flops 12891193344 | bytes 38797312 | tf_op jit(solution)/shard_map/dot_general | solution.py:246
  518.4 2.3 copy-done.1
  520.7 2.3 copy-done.5
  522.9 1.6 copy-done.7
  524.6 5.6 norm_bwd.2
  530.2 0.6 reduce-scatter.9.cloned.1.call-done.dh_ref
  530.9 2.2 copy-done.2
  533.0 2.2 copy-done.6
  535.2 1.6 copy-done.10
  536.8 5.6 norm_bwd.3
  542.5 78.0 %reduce-scatter.7.cloned.1.call-done.o_ref = bf16[256,4096]{1,0:T(8,128)(2,1)} async-done(((bf16[2048,4096]{1,0:T(8,128)(2,1)}), bf16[256,4096]{1,0:T(8,128)(2,1)}) %reduce-scatter.7.cloned.1.call-update) | async-done | bytes 2097168 | tf_op jit(solution)/shard_map/reduce_scatter | solution.py:260
  620.5 2.2 copy-done.3
  622.7 1.6 copy-done.8
  624.3 2.0 residual.2.refs_0_
  626.3 25.5 %psum.7 = bf16[4096]{0:T(1024)(128)(2,1)} all-reduce(f32[4096]{0:T(1024)S(1)} %bitcast.63), channel_id=1, replica_groups=mesh['dp'=2,'tp'=8] {'tp'}, use_global_device_ids=true, to_apply=%region_6.0 | all-reduce | flops 4096 | bytes 24576 | tf_op jit(solution)/shard_map/psum | solution.py:298
  651.8 58.7 %reduce-scatter.5.cloned.1.call-done.o_ref = bf16[256,4096]{1,0:T(8,128)(2,1)} async-done(((bf16[2048,4096]{1,0:T(8,128)(2,1)}), bf16[256,4096]{1,0:T(8,128)(2,1)}) %reduce-scatter.5.cloned.1.call-update) | async-done | bytes 2097168 | tf_op jit(solution)/shard_map/reduce_scatter | solution.py:260
  710.5 2.2 copy-done.4
  712.7 1.6 copy-done.9
  714.3 2.0 residual.3
  (51 shorter events, 0.4 us)
Async XLA Ops:
  7.2 93.5 %all-gather.11.cloned.1.call-start = ((), (), s32[]{:S(2)}) async-start(), calls=%async_computation.9 | async-start | bytes 18874368 | tf_op jit(solution)/shard_map/all_gather | solution.py:257
  7.2 3.5 copy-start
  7.3 4.7 copy-start.27
  12.0 2.3 copy-start.11
  16.9 167.5 %all-gather.13.cloned.1.call-start = ((), (), s32[]{:S(2)}) async-start(), calls=%async_computation.10 | async-start | bytes 18874368 | tf_op jit(solution)/shard_map/all_gather | solution.py:257
  21.7 246.2 %all-gather.9.cloned.1.call-start = ((), (), s32[]{:S(2)}) async-start(), calls=%async_computation.8 | async-start | bytes 18874368 | tf_op jit(solution)/shard_map/all_gather | solution.py:257
  22.5 328.3 %all-gather.15.cloned.1.call-start = ((), (), s32[]{:S(2)}) async-start(), calls=%async_computation.11 | async-start | bytes 18874368 | tf_op jit(solution)/shard_map/all_gather | solution.py:257
  23.2 495.2 %reduce-scatter.11.cloned.1.call-start = ((), (), s32[]{:S(2)}) async-start(), calls=%async_computation.7 | async-start | bytes 18874368 | tf_op jit(solution)/shard_map/reduce_scatter | solution.py:260
  118.9 30.4 %copy-start.23 = (bf16[2048,768]{1,0:T(8,128)(2,1)}, bf16[2048,768]{1,0:T(8,128)(2,1)S(1)}, u32[]{:S(2)}) copy-start(bf16[2048,768]{1,0:T(8,128)(2,1)S(1)} %fusion.34.q_ref.k_ref.v_ref) | copy-start | bytes 9437188
  118.9 30.4 %copy-start.28 = (bf16[512,4096]{1,0:T(8,128)(2,1)S(1)}, bf16[512,4096]{1,0:T(8,128)(2,1)}, u32[]{:S(2)}) copy-start(bf16[512,4096]{1,0:T(8,128)(2,1)} %param.8) | copy-start | bytes 12582916
  161.0 1.4 copy-start.13
  184.3 13.8 %copy-start.14 = (bf16[2048,512]{1,0:T(8,128)(2,1)S(1)}, bf16[2048,512]{1,0:T(8,128)(2,1)}, u32[]{:S(2)}) copy-start(bf16[2048,512]{1,0:T(8,128)(2,1)} %copy-done.13) | copy-start | bytes 6291460
  184.3 13.8 %copy-start.24 = (bf16[2048,768]{1,0:T(8,128)(2,1)S(1)}, bf16[2048,768]{1,0:T(8,128)(2,1)}, u32[]{:S(2)}) copy-start(bf16[2048,768]{1,0:T(8,128)(2,1)} %copy-done.23) | copy-start | bytes 9437188
  238.1 1.7 copy-start.19
  258.6 272.3 %reduce-scatter.9.cloned.1.call-start = ((), (), s32[]{:S(2)}) async-start(), calls=%async_computation.6 | async-start | bytes 18874368 | tf_op jit(solution)/shard_map/reduce_scatter | solution.py:260
  316.4 1.3 copy-start.16
  317.7 1.7 copy-start.25
  350.8 13.8 %copy-start.17 = (bf16[2048,512]{1,0:T(8,128)(2,1)S(1)}, bf16[2048,512]{1,0:T(8,128)(2,1)}, u32[]{:S(2)}) copy-start(bf16[2048,512]{1,0:T(8,128)(2,1)} %copy-done.16) | copy-start | bytes 6291460
  350.8 13.8 %copy-start.26 = (bf16[2048,768]{1,0:T(8,128)(2,1)S(1)}, bf16[2048,768]{1,0:T(8,128)(2,1)}, u32[]{:S(2)}) copy-start(bf16[2048,768]{1,0:T(8,128)(2,1)} %copy-done.25) | copy-start | bytes 9437188
  404.8 1.7 copy-start.21
  425.3 1.7 copy-start.18
  425.3 195.2 %reduce-scatter.7.cloned.1.call-start = ((), (), s32[]{:S(2)}) async-start(), calls=%async_computation.5 | async-start | bytes 18874368 | tf_op jit(solution)/shard_map/reduce_scatter | solution.py:260
  426.1 284.4 %reduce-scatter.5.cloned.1.call-start = ((), (), s32[]{:S(2)}) async-start(), calls=%async_computation.4 | async-start | bytes 18874368 | tf_op jit(solution)/shard_map/reduce_scatter | solution.py:260
  441.1 14.7 %copy-start.15 = (bf16[2048,512]{1,0:T(8,128)(2,1)S(1)}, bf16[2048,512]{1,0:T(8,128)(2,1)}, u32[]{:S(2)}) copy-start(bf16[2048,512]{1,0:T(8,128)(2,1)} %copy-done.13) | copy-start | bytes 6291460
  455.8 17.5 %copy-start.22 = (bf16[2048,768]{1,0:T(8,128)(2,1)S(1)}, bf16[2048,768]{1,0:T(8,128)(2,1)}, u32[]{:S(2)}) copy-start(bf16[2048,768]{1,0:T(8,128)(2,1)} %copy-done.21) | copy-start | bytes 9437188
  473.3 20.3 %copy-start.20 = (bf16[2048,768]{1,0:T(8,128)(2,1)S(1)}, bf16[2048,768]{1,0:T(8,128)(2,1)}, u32[]{:S(2)}) copy-start(bf16[2048,768]{1,0:T(8,128)(2,1)} %copy-done.19) | copy-start | bytes 9437188
  493.6 24.8 %copy-start.12 = (f32[4096]{0:T(1024)S(1)}, f32[4096]{0:T(1024)}, u32[]{:S(2)}) copy-start(f32[4096]{0:T(1024)} %copy-done.11) | copy-start | bytes 49156
  518.4 2.3 copy-start.1
  520.7 2.3 copy-start.5
  522.9 1.6 copy-start.7
  530.9 2.2 copy-start.2
  533.0 2.2 copy-start.6
  535.2 1.6 copy-start.10
  620.5 2.2 copy-start.3
  622.7 1.6 copy-start.8
  710.5 2.2 copy-start.4
  712.7 1.6 copy-start.9
Sparse Core Ops, SparseCore 0:
  17.0 83.6 all-gather.10
  102.9 81.3 all-gather.12
  186.5 81.3 all-gather.8
  269.4 81.3 all-gather.14
  353.0 88.2 reduce-scatter.10
  443.5 87.2 reduce-scatter.8
  533.2 87.2 reduce-scatter.6
  622.9 87.5 reduce-scatter.4
